TPU v7x, 128 devices: a whole 4x4x4 slice. The times are simulated.
128 devices in a mesh: rep: 1, data: 2 (over core), model: 64 (over z, y, x).
Axes of the slice: x: 4, y: 4, z: 4, core: 2. Of those that a mesh axis runs over, the one named last changes fastest.
Arguments:
- x: bfloat16 [4, 2048, 1024], P(('rep', 'data'), 'model')
- lengths: int32 [4], P(('rep', 'data'))
- gamma: bfloat16 [2, 1024], P(None, 'data')
- w_in: bfloat16 [2, 1024, 147456], P(None, 'data', 'model')
- w_kv: bfloat16 [2, 1024, 256], P(None, 'data')
- w_out: bfloat16 [2, 81920, 1024], P(None, 'model', 'data')
Outputs:
- output: bfloat16 [4, 2048, 1024], P(('rep', 'data'), 'model')
All inputs are finite; a program needn't handle non-finite values.
Results may differ from a plain program's by a relative error of at most 0.02.
Values are sent between devices in bfloat16 or wider.
A program may use at most 1 GiB of HBM per device.

v0:
```python
import jax
import jax.numpy as jnp
from jax import lax
from jax.sharding import PartitionSpec as P

EPSILON = 1e-6


def rms_norm(x_in, gain):
    x_f32 = x_in.astype(jnp.float32)
    inv_rms = lax.rsqrt(jnp.mean(x_f32 * x_f32, axis=-1, keepdims=True) + EPSILON)
    return (x_f32 * inv_rms * gain.astype(jnp.float32)).astype(jnp.bfloat16)


def attend(queries, keys, values, seq_lens, q_offset, block_len):
    n_batch, n_query, n_heads, head_dim = queries.shape
    n_blocks = n_query // block_len
    q_blocks = queries.reshape(n_batch, n_blocks, block_len, n_heads, head_dim)
    key_pos = jnp.arange(keys.shape[1])

    def one_block(blk_idx):
        q_blk = lax.dynamic_index_in_dim(q_blocks, blk_idx, axis=1, keepdims=False)
        scores = jnp.einsum("crie,cle->cirl", q_blk, keys, preferred_element_type=jnp.float32) * (head_dim ** -0.5)
        q_pos = q_offset + blk_idx * block_len + jnp.arange(block_len)
        visible = (key_pos[None, None, :] <= q_pos[None, :, None]) & (key_pos[None, None, :] < seq_lens[:, None, None])
        scores = jnp.where(visible[:, None], scores, -1e30)
        attn_probs = jax.nn.softmax(scores, axis=-1).astype(jnp.bfloat16)
        blk_out = jnp.einsum("cirl,cle->crie", attn_probs, values, preferred_element_type=jnp.float32)
        return blk_out.astype(jnp.bfloat16).reshape(n_batch, block_len, n_heads * head_dim)

    return lax.map(one_block, jnp.arange(n_blocks))


def solution(mesh):
    batch_axes = ("rep", "data")

    def local_step(x_loc, lens_loc, gamma_loc, w_in_loc, w_kv_loc, w_out_loc):
        n_batch, seq_loc, d_model = x_loc.shape
        head_dim = w_kv_loc.shape[2] // 2
        in_local = w_in_loc.shape[2]
        out_local = w_out_loc.shape[1]
        ff_local = in_local - out_local
        attn_cols = out_local - ff_local
        hidden = x_loc
        for layer in range(gamma_loc.shape[0]):
            gain = lax.all_gather(gamma_loc[layer], "data", axis=0, tiled=True)
            w_in_full = lax.all_gather(w_in_loc[layer], "data", axis=0, tiled=True)
            w_kv_full = lax.all_gather(w_kv_loc[layer], "data", axis=0, tiled=True)
            w_out_full = lax.all_gather(w_out_loc[layer], "data", axis=1, tiled=True)
            normed = rms_norm(hidden, gain)
            h_full = lax.all_gather(normed, "model", axis=1, tiled=True)
            seq_len = h_full.shape[1]
            projected = jnp.einsum("btd,dc->btc", h_full, w_in_full, preferred_element_type=jnp.float32).astype(jnp.bfloat16)
            key_value = jnp.einsum("btd,de->bte", h_full, w_kv_full, preferred_element_type=jnp.float32).astype(jnp.bfloat16)
            queries = projected[:, :, :attn_cols].reshape(n_batch, seq_len, attn_cols // head_dim, head_dim)
            attn_blocks = attend(queries, key_value[:, :, :head_dim], key_value[:, :, head_dim:], lens_loc, 0, seq_loc)
            gate = projected[:, :, attn_cols:attn_cols + ff_local].astype(jnp.float32)
            up_proj = projected[:, :, attn_cols + ff_local:].astype(jnp.float32)
            mlp_out = (jax.nn.silu(gate) * up_proj).astype(jnp.bfloat16)
            z_attn = jnp.einsum("nbqe,ed->bnqd", attn_blocks, w_out_full[:attn_cols], preferred_element_type=jnp.float32).reshape(n_batch, seq_len, d_model)
            z_mlp = jnp.einsum("btf,fd->btd", mlp_out, w_out_full[attn_cols:], preferred_element_type=jnp.float32)
            z_part = (z_attn + z_mlp).astype(jnp.bfloat16)
            z_sum = lax.psum_scatter(z_part, "model", scatter_dimension=1, tiled=True)
            hidden = (hidden.astype(jnp.float32) + z_sum.astype(jnp.float32)).astype(jnp.bfloat16)
        return hidden

    in_specs = (
        P(batch_axes, "model", None),
        P(batch_axes),
        P(None, "data"),
        P(None, "data", "model"),
        P(None, "data", None),
        P(None, "model", "data"),
    )
    return jax.shard_map(local_step, mesh=mesh, in_specs=in_specs, out_specs=P(batch_axes, "model", None), check_vma=False)
```

profile of v0, /device:TPU:0, one launch (start us, length us, event | category | flops | bytes accessed | tf_op | source)
XLA Modules:
  0.0 1970.8 jit_solution(8657560455999963366)
XLA Ops:
  6.5 4.8 fusion.60
  11.5 1.9 all-gather
  14.4 3.4 fusion.61
  17.9 2.2 all-gather.2
  20.1 11.5 all-gather.19.cloned.1.call-done
  31.6 83.0 %all-gather.15.cloned.1.call-done = bf16[2,2048,1024]{2,1,0:T(8,128)(2,1)} async-done(((bf16[2,32,1024]{2,1,0:T(8,128)(2,1)}), bf16[2,2048,1024]{2,1,0:T(8,128)(2,1)}) %all-gather.15.cloned.1.call-update) | async-done | bytes 8388624 | tf_op jit(solution)/shard_map/all_gather | solution.py:51
  114.6 26.8 %convolution_convert_fusion.3 = bf16[2,2048,2304]{2,1,0:T(8,128)(2,1)} fusion(bf16[2,2048,1024]{2,1,0:T(8,128)(2,1)} %all-gather.15.cloned.1.call-done, bf16[1,1024,2304]{2,1,0:T(8,128)(2,1)} %all-gather.19.cloned.1.call-done), kind=kOutput, calls=%fused_computation.61 | convolution fusion | flops 19336790016 | bytes 31981568 | tf_op jit(solution)/shard_map/btd,dc->btc/dot_general | solution.py:53
  142.9 2.1 reshape_reshape.6
  145.0 5.7 convolution_convert_fusion.5
  153.7 475.6 %while.24 = (s32[]{:T(128)}, bf16[64,2,32,256]{3,2,1,0:T(8,128)(2,1)}, s32[64]{0:T(128)S(1)}, s32[2]{0:T(128)S(1)}, bf16[2,64,32,2,128]{4,3,2,1,0:T(2,128)(2,1)}...) while((s32[]{:T(128)}, ...), condition=%wide.region_4.5_spmd.clone.clone, body=%wide.region_1.4_spmd.clone.clone.sunk | while | flops 136274080 | bytes 5973943 | solution.py:31
  218.2 1.7 fusion.96
  225.7 1.7 fusion.96
  247.9 1.7 fusion.96
  270.2 1.7 fusion.96
  285.1 1.7 fusion.96
  337.1 1.7 fusion.96
  352.0 1.7 fusion.96
  366.8 1.7 fusion.96
  381.7 1.7 fusion.96
  389.1 1.7 fusion.96
  404.0 1.7 fusion.96
  418.8 1.7 fusion.96
  441.1 1.7 fusion.96
  485.7 1.7 fusion.96
  500.6 1.7 fusion.96
  522.8 1.7 fusion.96
  530.3 1.7 fusion.96
  545.1 1.7 fusion.96
  567.4 1.7 fusion.96
  574.9 1.7 fusion.96
  597.1 1.7 fusion.96
  626.9 1.7 fusion.96
  629.4 4.0 convolution_bitcast_fusion.1
  633.4 6.1 copy.14
  639.5 19.8 %fusion.33 = bf16[2,2048,1024]{2,1,0:T(8,128)(2,1)} fusion(f32[2,64,32,1024]{3,2,1,0:T(8,128)} %copy.14, bf16[2,2048,2304]{2,1,0:T(8,128)(2,1)} %convolution_convert_fusion.3, bf16[1,1280,1024]{2,1,0:T(8,128)(2,1)} %all-gather.21.cloned.1.call-done), kind=kOutput, calls=%fused_computation.57 | convolution fusion | flops 8631877632 | bytes 44040192 | tf_op jit(solution)/shard_map/btf,fd->btd/dot_general | solution.py:61
  660.0 1.8 all-gather.4
  661.8 367.5 %reduce-scatter.3.cloned.1.call-done = bf16[2,32,1024]{2,1,0:T(8,128)(2,1)} async-done(((bf16[2,2048,1024]{2,1,0:T(8,128)(2,1)}), bf16[2,32,1024]{2,1,0:T(8,128)(2,1)}) %reduce-scatter.3.cloned.1.call-update) | async-done | bytes 131088 | tf_op jit(solution)/shard_map/reduce_scatter | solution.py:63
  1032.8 2.2 all-gather.6
  1035.0 8.1 all-gather.23.cloned.1.call-done
  1043.1 82.8 %all-gather.17.cloned.1.call-done = bf16[2,2048,1024]{2,1,0:T(8,128)(2,1)} async-done(((bf16[2,32,1024]{2,1,0:T(8,128)(2,1)}), bf16[2,2048,1024]{2,1,0:T(8,128)(2,1)}) %all-gather.17.cloned.1.call-update) | async-done | bytes 8388624 | tf_op jit(solution)/shard_map/all_gather | solution.py:51
  1125.9 27.0 %convolution_convert_fusion.2 = bf16[2,2048,2304]{2,1,0:T(8,128)(2,1)} fusion(bf16[2,2048,1024]{2,1,0:T(8,128)(2,1)} %all-gather.17.cloned.1.call-done, bf16[1,1024,2304]{2,1,0:T(8,128)(2,1)} %all-gather.23.cloned.1.call-done), kind=kOutput, calls=%fused_computation.60 | convolution fusion | flops 19336790016 | bytes 31981568 | tf_op jit(solution)/shard_map/btd,dc->btc/dot_general | solution.py:53
  1154.5 2.1 reshape_reshape.7
  1156.5 5.7 convolution_convert_fusion.4
  1164.2 397.5 %while.25 = (s32[]{:T(128)}, bf16[64,2,32,256]{3,2,1,0:T(8,128)(2,1)}, s32[64]{0:T(128)S(1)}, s32[2]{0:T(128)S(1)}, bf16[2,64,32,2,128]{4,3,2,1,0:T(2,128)(2,1)}...) while((s32[]{:T(128)}, ...), condition=%wide.region_10.11_spmd.clone.clone, body=%wide.region_7.10_spmd.clone.clone.sunk | while | flops 136274080 | bytes 5973943 | solution.py:31
  1561.8 4.0 convolution_bitcast_fusion
  1565.8 6.1 copy.16
  1571.9 19.8 %fusion.32 = bf16[2,2048,1024]{2,1,0:T(8,128)(2,1)} fusion(f32[2,64,32,1024]{3,2,1,0:T(8,128)} %copy.16, bf16[2,2048,2304]{2,1,0:T(8,128)(2,1)} %convolution_convert_fusion.2, bf16[1,1280,1024]{2,1,0:T(8,128)(2,1)} %all-gather.25.cloned.1.call-done), kind=kOutput, calls=%fused_computation.55 | convolution fusion | flops 8631877632 | bytes 44040192 | tf_op jit(solution)/shard_map/btf,fd->btd/dot_general | solution.py:61
  1591.7 370.2 %reduce-scatter.5.cloned.1.call-done = bf16[2,32,1024]{2,1,0:T(8,128)(2,1)} async-done(((bf16[2,2048,1024]{2,1,0:T(8,128)(2,1)}), bf16[2,32,1024]{2,1,0:T(8,128)(2,1)}) %reduce-scatter.5.cloned.1.call-update) | async-done | bytes 131088 | tf_op jit(solution)/shard_map/reduce_scatter | solution.py:63
  (1563 shorter events, 512.3 us)
Async XLA Ops:
  6.5 4.9 copy-start.4
  6.5 6.9 copy-start
  6.5 25.0 %all-gather.19.cloned.1.call-start = ((), (), s32[]{:S(2)}) async-start(), calls=%async_computation.6 | async-start | bytes 7077888 | tf_op jit(solution)/shard_map/all_gather | solution.py:47
  11.3 6.5 copy-start.2
  11.4 103.2 %all-gather.15.cloned.1.call-start = ((), (), s32[]{:S(2)}) async-start(), calls=%async_computation.2 | async-start | bytes 8519680 | tf_op jit(solution)/shard_map/all_gather | solution.py:51
  14.3 615.1 %all-gather.21.cloned.1.call-start = ((), (), s32[]{:S(2)}) async-start(), calls=%async_computation.7 | async-start | bytes 3932160 | tf_op jit(solution)/shard_map/all_gather | solution.py:49
  17.8 1011.5 %reduce-scatter.3.cloned.1.call-start = ((), (), s32[]{:S(2)}) async-start(), calls=%async_computation.3 | async-start | bytes 8519680 | tf_op jit(solution)/shard_map/reduce_scatter | solution.py:63
  141.3 1.6 slice-start
  150.7 3.0 copy-start.3
  659.4 383.7 %all-gather.23.cloned.1.call-start = ((), (), s32[]{:S(2)}) async-start(), calls=%async_computation.8 | async-start | bytes 7077888 | tf_op jit(solution)/shard_map/all_gather | solution.py:47
  659.9 466.0 %all-gather.17.cloned.1.call-start = ((), (), s32[]{:S(2)}) async-start(), calls=%async_computation.4 | async-start | bytes 8519680 | tf_op jit(solution)/shard_map/all_gather | solution.py:51
  1032.0 529.7 %all-gather.25.cloned.1.call-start = ((), (), s32[]{:S(2)}) async-start(), calls=%async_computation.9 | async-start | bytes 3932160 | tf_op jit(solution)/shard_map/all_gather | solution.py:49
  1032.8 929.1 %reduce-scatter.5.cloned.1.call-start = ((), (), s32[]{:S(2)}) async-start(), calls=%async_computation.5 | async-start | bytes 8519680 | tf_op jit(solution)/shard_map/reduce_scatter | solution.py:63
  1152.9 1.6 slice-start.1
  1591.7 370.2 %copy-start.1 = (bf16[2,32,1024]{2,1,0:T(8,128)(2,1)S(1)}, bf16[2,32,1024]{2,1,0:T(8,128)(2,1)}, u32[]{:S(2)}) copy-start(bf16[2,32,1024]{2,1,0:T(8,128)(2,1)} %reduce-scatter.3.cloned.1.call-done) | copy-start | bytes 393220
Sparse Core Ops, SparseCore 0:
  11.5 20.0 all-gather.18
  34.5 80.0 all-gather.14
  116.2 13.6 all-gather.20
  659.5 369.8 reduce-scatter.2
  1030.8 12.2 all-gather.22
  1045.8 80.0 all-gather.16
  1127.6 13.6 all-gather.24
  1591.9 370.0 reduce-scatter.4
where the time goes:
time: 2000 us; the launch traced here: 1970 us
  waiting for transfers between devices  924 us (46%)
  loops' own time  339 us (17%)
  matrix products  311 us (16%)
  local copies, waits for them, and re-layouts  293 us (15%)
  other arithmetic  80.4 us (4%)
    reduce_scatter x2, waiting for transfers between devices, local_step(): z_sum = lax.psum_scatter(z_part, 'model', scatter_dimension=1, tiled=True)  738 us
    another operation x2, loops' own time, attend(): return lax.map(one_block, jnp.arange(n_blocks))  339 us
    all_gather x2, waiting for transfers between devices, local_step(): h_full = lax.all_gather(normed, 'model', axis=1, tiled=True)  166 us
    dot_general x128, matrix products, one_block(): jnp.einsum('cirl,cle->crie', attn_probs, values, preferred_element_type=j...  136 us
    dynamic_slice x128, local copies, waits for them, and re-layouts, one_block(): q_blk = lax.dynamic_index_in_dim(q_blocks, blk_idx, axis=1, keepdims=False)  101 us
    dynamic_update_slice x128, local copies, waits for them, and re-layouts, attend(): return lax.map(one_block, jnp.arange(n_blocks))  78 us
    dynamic_slice x128, local copies, waits for them, and re-layouts, attend(): return lax.map(one_block, jnp.arange(n_blocks))  74.5 us
    dot_general x128, matrix products, one_block(): jnp.einsum('crie,cle->cirl', q_blk, keys, preferred_element_type=jnp.floa...  61.8 us
  transfers between devices with their start and end apart: 8, of which 6 were waited for; matrix products, arithmetic and copies ran while one was open for 31% of the time, Pallas kernels for 0%

commit v1 on v0

v1 whole, which is shorter than its diff:
```python
import functools

import jax
import jax.numpy as jnp
from jax import lax
from jax.experimental import pallas as pl
from jax.experimental.pallas import tpu as pltpu
from jax.sharding import PartitionSpec as P

EPSILON = 1e-6
MESH = pl.DeviceIdType.MESH
F32 = jnp.float32
BF16 = jnp.bfloat16

SIDE = 4
ROWS = 32
D_MODEL = 1024
HEAD = 128
ATTN = 256
FF = 1024
TILE = SIDE * SIDE * ROWS
N_TILES = SIDE
STRIDE = (16, 4, 1)
COLS = ((0, 384), (384, 384), (768, 256))
AG_ORDER = ((2, 1, 0), (1, 0, 2), (0, 2, 1))
RS_ORDER = tuple(tuple(reversed(order)) for order in AG_ORDER)
POINTS = 6
NEG = -1e30


def kernel(
    x_ref, len_ref, gamma_ref, w_in_ref, w_kv_ref, w_out_ref, y_ref,
    win, wkv, wout, gfull, hbuf, zbuf, xcur,
    ra0, ra1, ra2, rb0, rb1, rb2,
    k_t, v_ext, q_ext, acc, row_max, mixed,
    ag_send, ag_recv, rs_send, rs_recv, w_local, w_send, w_recv, g_local, g_send, g_recv,
):
    m = lax.axis_index("model")
    core = lax.axis_index("data")
    other = 1 - core
    pos = (lax.div(m, 16), lax.rem(lax.div(m, 4), 4), lax.rem(m, 4))
    ra = (ra0, ra1, ra2)
    rb = (rb0, rb1, rb2)

    def shift(axis, delta):
        return lax.rem(pos[axis] + delta + SIDE, SIDE)

    def neighbour(axis, delta):
        return {"model": m + (shift(axis, delta) - pos[axis]) * STRIDE[axis]}

    barrier = pltpu.get_barrier_semaphore()
    for axis in range(3):
        for delta in (1, -1):
            pl.semaphore_signal(barrier, inc=1, device_id=neighbour(axis, delta), device_id_type=MESH)
    pl.semaphore_signal(barrier, inc=1, device_id={"data": other}, device_id_type=MESH)
    pl.semaphore_wait(barrier, 7)

    pairs = ((w_in_ref, win), (w_kv_ref, wkv), (w_out_ref, wout))

    def weight_local(layer, i):
        src, dst = pairs[i]
        return pltpu.make_async_copy(src.at[layer], dst.at[layer, core], w_local.at[layer, i])

    def weight_send(layer, i):
        src, dst = pairs[i]
        return pltpu.make_async_remote_copy(
            src_ref=src.at[layer], dst_ref=dst.at[layer, core], send_sem=w_send.at[layer, i],
            recv_sem=w_recv.at[layer, i], device_id={"data": other}, device_id_type=MESH)

    def weight_arrival(layer, i):
        src, dst = pairs[i]
        return pltpu.make_async_remote_copy(
            src_ref=src.at[layer], dst_ref=dst.at[layer, other], send_sem=w_send.at[layer, i],
            recv_sem=w_recv.at[layer, i], device_id={"data": other}, device_id_type=MESH)

    def weights_start(layer):
        for i in range(3):
            weight_send(layer, i).start()
            weight_local(layer, i).start()

    def weights_wait(layer):
        for i in range(3):
            weight_local(layer, i).wait()
            weight_send(layer, i).wait_send()
            weight_arrival(layer, i).wait_recv()

    gain_local = pltpu.make_async_copy(gamma_ref, gfull.at[core], g_local)
    gain_send = pltpu.make_async_remote_copy(
        src_ref=gamma_ref, dst_ref=gfull.at[core], send_sem=g_send, recv_sem=g_recv,
        device_id={"data": other}, device_id_type=MESH)
    gain_arrival = pltpu.make_async_remote_copy(
        src_ref=gamma_ref, dst_ref=gfull.at[other], send_sem=g_send, recv_sem=g_recv,
        device_id={"data": other}, device_id_type=MESH)
    gain_send.start()
    gain_local.start()
    weights_start(0)

    def h_block(b, part, phase, index, rows):
        order = AG_ORDER[part]
        where = [slice(None)] * 3
        for axis in order[phase + 1:]:
            where[axis] = pos[axis]
        where[order[phase]] = index
        lo, width = COLS[part]
        return hbuf.at[(b, *where, pl.ds(*rows), pl.ds(lo, width))]

    HALVES = ((0, ROWS // 2), (ROWS // 2, ROWS // 2))
    WHOLE = (0, ROWS)

    def ag_copy(b, part, phase, slot, index, rows, delta):
        block = h_block(b, part, phase, index, rows)
        return pltpu.make_async_remote_copy(
            src_ref=block, dst_ref=block, send_sem=ag_send.at[b, part, phase, slot],
            recv_sem=ag_recv.at[b, part, phase, slot],
            device_id=neighbour(AG_ORDER[part][phase], delta), device_id_type=MESH)

    def ag_sent(b, part, phase, slot):
        axis = AG_ORDER[part][phase]
        if slot == 0:
            return ag_copy(b, part, phase, 0, pos[axis], WHOLE, 1)
        if slot == 1:
            return ag_copy(b, part, phase, 1, pos[axis], WHOLE, -1)
        if slot == 2:
            return ag_copy(b, part, phase, 2, shift(axis, -1), HALVES[0], 1)
        return ag_copy(b, part, phase, 3, shift(axis, 1), HALVES[1], -1)

    def ag_arrival(b, part, phase, slot):
        axis = AG_ORDER[part][phase]
        if slot == 0:
            return ag_copy(b, part, phase, 0, shift(axis, -1), WHOLE, 1)
        if slot == 1:
            return ag_copy(b, part, phase, 1, shift(axis, 1), WHOLE, -1)
        if slot == 2:
            return ag_copy(b, part, phase, 2, shift(axis, 2), HALVES[0], 1)
        return ag_copy(b, part, phase, 3, shift(axis, 2), HALVES[1], -1)

    def ag_step(b, stage):
        phase, second = stage // 2, stage % 2
        for part in range(3):
            if stage:
                before, was_second = (stage - 1) // 2, (stage - 1) % 2
                for slot in ((2, 3) if was_second else (0, 1)):
                    ag_arrival(b, part, before, slot).wait_recv()
            if stage < 6:
                for slot in ((2, 3) if second else (0, 1)):
                    ag_sent(b, part, phase, slot).start()
        if stage == 6:
            for part in range(3):
                for k in range(3):
                    for slot in range(4):
                        ag_sent(b, part, k, slot).wait_send()

    def z_where(b, part, phase, index):
        order = RS_ORDER[part]
        where = [None] * 3
        for axis in order[:phase]:
            where[axis] = pos[axis]
        where[order[phase]] = index
        return where

    def z_block(b, part, phase, index, rows):
        where = [slice(None) if i is None else i for i in z_where(b, part, phase, index)]
        lo, width = COLS[part]
        return zbuf.at[(b, *where, pl.ds(*rows), pl.ds(lo, width))]

    def r_block(buf, b, part, phase, side, rows):
        lo, width = COLS[part]
        return buf[phase].at[(b, side, *([slice(None)] * (2 - phase)), pl.ds(*rows), pl.ds(lo, width))]

    def rs_copy(b, part, phase, slot):
        axis = RS_ORDER[part][phase]
        if slot == 0:
            src = z_block(b, part, phase, shift(axis, 2), HALVES[0])
            dst, delta = r_block(ra, b, part, phase, 0, (0, ROWS // 2)), -1
        elif slot == 1:
            src = z_block(b, part, phase, shift(axis, 2), HALVES[1])
            dst, delta = r_block(ra, b, part, phase, 1, (0, ROWS // 2)), 1
        elif slot == 2:
            src = z_block(b, part, phase, shift(axis, -1), WHOLE)
            dst, delta = r_block(rb, b, part, phase, 0, WHOLE), -1
        else:
            src = z_block(b, part, phase, shift(axis, 1), WHOLE)
            dst, delta = r_block(rb, b, part, phase, 1, WHOLE), 1
        return pltpu.make_async_remote_copy(
            src_ref=src, dst_ref=dst, send_sem=rs_send.at[b, part, phase, slot],
            recv_sem=rs_recv.at[b, part, phase, slot],
            device_id=neighbour(axis, delta), device_id_type=MESH)

    def add_into(b, part, phase, index, rows, sources):
        where = z_where(b, part, phase, index)
        free = [i for i in range(3) if where[i] is None]
        lo, width = COLS[part]

        def one(i):
            at = list(where)
            lead = ()
            if free:
                at[free[0]] = i
                lead = (i,)
            at = [slice(None) if j is None else j for j in at]
            target = (b, *at, pl.ds(*rows), pl.ds(lo, width))
            total = zbuf[target].astype(F32)
            for buf, side in sources:
                rest = [slice(None)] * (len(free) - len(lead))
                height = rows[1]
                total = total + buf[phase][(b, side, *lead, *rest, pl.ds(0, height), pl.ds(lo, width))].astype(F32)
            zbuf[target] = total.astype(BF16)

        if len(free) == 2:
            @pl.loop(0, SIDE)
            def _(i):
                one(i)
        elif len(free) == 1:
            for i in range(SIDE):
                one(i)
        else:
            one(None)

    def rs_step(b, stage):
        phase, second = stage // 2, stage % 2
        for part in range(3):
            if stage:
                before, was_second = (stage - 1) // 2, (stage - 1) % 2
                axis = RS_ORDER[part][before]
                for slot in ((2, 3) if was_second else (0, 1)):
                    rs_copy(b, part, before, slot).wait_recv()
                if was_second:
                    add_into(b, part, before, pos[axis], WHOLE, ((rb, 0), (rb, 1)))
                else:
                    add_into(b, part, before, shift(axis, -1), HALVES[0], ((ra, 0),))
                    add_into(b, part, before, shift(axis, 1), HALVES[1], ((ra, 1),))
            if stage < 6:
                for slot in ((2, 3) if second else (0, 1)):
                    rs_copy(b, part, phase, slot).start()
        if stage == 6:
            for part in range(3):
                for k in range(3):
                    for slot in range(4):
                        rs_copy(b, part, k, slot).wait_send()

    def norm(b, layer):
        x = xcur[b].astype(F32)
        gain = jnp.concatenate([gfull[0, layer:layer + 1, :], gfull[1, layer:layer + 1, :]], axis=1).astype(F32)
        inv = lax.rsqrt(jnp.mean(x * x, axis=-1, keepdims=True) + EPSILON)
        hbuf[b, pos[0], pos[1], pos[2]] = (x * inv * gain).astype(BF16)

    def residual(b):
        z = zbuf[b, pos[0], pos[1], pos[2]].astype(F32)
        xcur[b] = (xcur[b].astype(F32) + z).astype(BF16)

    xcur[...] = x_ref[...]
    gain_local.wait()
    gain_send.wait_send()
    gain_arrival.wait_recv()
    norm(0, 0)
    ag_step(0, 0)
    norm(1, 0)
    rows_i = lax.broadcasted_iota(jnp.int32, (HEAD, TILE), 0)
    q_ext[:, HEAD:] = jnp.where(lax.broadcasted_iota(jnp.int32, (2 * TILE, HEAD), 1) == 0, 1.0, 0.0).astype(BF16)
    v_ext[:, :, HEAD:] = jnp.ones((N_TILES, TILE, HEAD), BF16)
    for stage in range(1, 6):
        ag_step(0, stage)
    ag_step(1, 0)
    ag_step(0, 6)
    weights_wait(0)
    weights_start(1)

    plan = {}

    def at(seg, tick, kind, b, stage):
        plan.setdefault(divmod(seg * N_TILES * POINTS + tick, POINTS), []).append((kind, b, stage))

    for stage, tick in zip(range(1, 7), (2, 4, 7, 9, 17, 22)):
        at(0, tick, "ag", 1, stage)
    for stage, tick in zip(range(0, 7), (0, 4, 10, 12, 14, 16, 18)):
        at(1, tick, "rs", 0, stage)
    at(1, 18, "turn", 0, 0)
    for stage, tick in zip(range(0, 3), (18, 20, 22)):
        at(1, tick, "ag", 0, stage)
    at(2, 0, "rs", 1, 0)
    for stage in range(3, 7):
        at(2, 0, "ag", 0, stage)
    at(2, 0, "weights", 0, 1)
    for stage, tick in zip(range(1, 7), (1, 6, 8, 10, 12, 14)):
        at(2, tick, "rs", 1, stage)
    at(2, 14, "turn", 1, 0)
    for stage, tick in zip(range(0, 5), (14, 16, 18, 21, 23)):
        at(2, tick, "ag", 1, stage)
    at(3, 0, "rs", 0, 0)
    for stage in range(5, 7):
        at(3, 0, "ag", 1, stage)
    for stage, tick in zip(range(1, 7), (4, 11, 13, 15, 17, 19)):
        at(3, tick, "rs", 0, stage)

    def run(kind, b, stage):
        if kind == "ag":
            ag_step(b, stage)
        elif kind == "rs":
            rs_step(b, stage)
        elif kind == "weights":
            weights_wait(stage)
        else:
            residual(b)
            norm(b, 1)

    scale = float(HEAD ** -0.5 * 1.4426950408889634)
    CHUNK = 256

    def attend(j, diag):
        for lo in range(0, 2 * TILE, CHUNK):
            rows = pl.ds(lo, CHUNK)
            s = jnp.dot(q_ext[rows, :], k_t[j], preferred_element_type=F32)
            if diag:
                q_pos = (lo % TILE) + lax.broadcasted_iota(jnp.int32, (CHUNK, TILE), 0)
                s = jnp.where(lax.broadcasted_iota(jnp.int32, (CHUNK, TILE), 1) <= q_pos, s, NEG)
            top = jnp.max(s, axis=-1, keepdims=True)
            if diag:
                new = top
            else:
                old = row_max[rows, :1]
                new = jnp.maximum(old, top)
            p = jnp.exp2((s - new) * scale).astype(BF16)
            out = jnp.dot(p, v_ext[j], preferred_element_type=F32)
            if diag:
                acc[rows, :] = out
            else:
                acc[rows, :] = acc[rows, :] * jnp.exp2((old - new) * scale) + out
            row_max[rows, :] = jnp.broadcast_to(new, (CHUNK, HEAD))

    @pl.loop(0, 4 * N_TILES)
    def _(it):
        seg, t = lax.div(it, N_TILES), lax.rem(it, N_TILES)
        layer, b = lax.div(seg, 2), lax.rem(seg, 2)

        def tick(point):
            for (when, where), steps in plan.items():
                if where == point:
                    @pl.when(it == when)
                    def _(steps=steps):
                        for step in steps:
                            run(*step)

        tick(0)
        h = hbuf[b, t].reshape(TILE, D_MODEL)
        kv = jnp.dot(h, wkv[layer].reshape(D_MODEL, 2 * HEAD), preferred_element_type=F32).astype(BF16)
        k_t[t, :HEAD, :] = kv[:, :HEAD].T
        key_pos = t * TILE + lax.broadcasted_iota(jnp.int32, (HEAD, TILE), 1)
        hidden = jnp.logical_and(rows_i == 0, key_pos >= len_ref[pl.ds(b, 1), :])
        k_t[t, HEAD:, :] = jnp.where(hidden, NEG, 0.0).astype(BF16)
        v_ext[t, :, :HEAD] = kv[:, HEAD:]
        q = jnp.dot(h, win[layer, :, :, :ATTN].reshape(D_MODEL, ATTN), preferred_element_type=F32).astype(BF16)
        q_ext[:TILE, :HEAD] = q[:, :HEAD]
        q_ext[TILE:, :HEAD] = q[:, HEAD:]
        tick(1)
        for i in range(2):
            h = hbuf[b, t].reshape(TILE, D_MODEL)
            lo = ATTN + i * 512
            g = jnp.dot(h, win[layer, :, :, lo:lo + 512].reshape(D_MODEL, 512), preferred_element_type=F32)
            u = jnp.dot(h, win[layer, :, :, lo + FF:lo + FF + 512].reshape(D_MODEL, 512), preferred_element_type=F32)
            g = g.astype(BF16).astype(F32)
            u = u.astype(BF16).astype(F32)
            mixed[:, lo:lo + 512] = (jax.nn.silu(g) * u).astype(BF16)
            tick(2 + i)
        attend(t, True)
        tick(4)

        @pl.loop(0, N_TILES - 1)
        def _(j):
            @pl.when(j < t)
            def _():
                attend(j, False)

        for head in range(2):
            rows = pl.ds(head * TILE, TILE)
            mixed[:, head * HEAD:(head + 1) * HEAD] = (acc[rows, :HEAD] / acc[rows, HEAD:]).astype(BF16)
        tick(5)
        for half in range(2):
            z = jnp.dot(mixed[...], wout[layer, half], preferred_element_type=F32).astype(BF16)
            zbuf[b, t, :, :, :, half * 512:(half + 1) * 512] = z.reshape(SIDE, SIDE, ROWS, 512)

    rs_step(1, 0)
    residual(0)
    y_ref[0] = xcur[0]
    for stage in range(1, 7):
        rs_step(1, stage)
    residual(1)
    y_ref[1] = xcur[1]


def local_step(x, lengths, gamma, w_in, w_kv, w_out):
    vmem = pl.BlockSpec(memory_space=pltpu.VMEM)
    hbm = pl.BlockSpec(memory_space=pl.ANY)
    dma = pltpu.SemaphoreType.DMA
    box = (SIDE, SIDE)
    scratch = [
        pltpu.VMEM((2, 2, 512, 2304), BF16),
        pltpu.VMEM((2, 2, 512, 256), BF16),
        pltpu.VMEM((2, 2, 1280, 512), BF16),
        pltpu.VMEM((2, 2, 512), BF16),
        pltpu.VMEM((2, SIDE, *box, ROWS, D_MODEL), BF16),
        pltpu.VMEM((2, SIDE, *box, ROWS, D_MODEL), BF16),
        pltpu.VMEM((2, ROWS, D_MODEL), BF16),
        pltpu.VMEM((2, 2, *box, ROWS // 2, D_MODEL), BF16),
        pltpu.VMEM((2, 2, SIDE, ROWS // 2, D_MODEL), BF16),
        pltpu.VMEM((2, 2, ROWS // 2, D_MODEL), BF16),
        pltpu.VMEM((2, 2, *box, ROWS, D_MODEL), BF16),
        pltpu.VMEM((2, 2, SIDE, ROWS, D_MODEL), BF16),
        pltpu.VMEM((2, 2, ROWS, D_MODEL), BF16),
        pltpu.VMEM((N_TILES, 2 * HEAD, TILE), BF16),
        pltpu.VMEM((N_TILES, TILE, 2 * HEAD), BF16),
        pltpu.VMEM((2 * TILE, 2 * HEAD), BF16),
        pltpu.VMEM((2 * TILE, 2 * HEAD), F32),
        pltpu.VMEM((2 * TILE, HEAD), F32),
        pltpu.VMEM((TILE, ATTN + FF), BF16),
        dma((2, 3, 3, 4)), dma((2, 3, 3, 4)), dma((2, 3, 3, 4)), dma((2, 3, 3, 4)),
        dma((2, 3)), dma((2, 3)), dma((2, 3)), dma, dma, dma,
    ]
    return pl.pallas_call(
        kernel,
        out_shape=jax.ShapeDtypeStruct(x.shape, x.dtype),
        in_specs=[vmem, vmem, vmem, hbm, hbm, hbm],
        out_specs=vmem,
        scratch_shapes=scratch,
        compiler_params=pltpu.CompilerParams(
            collective_id=0, has_side_effects=True, vmem_limit_bytes=67_043_328),
        name="layers",
    )(x, lengths.reshape(2, 1), gamma, w_in, w_kv, w_out)


def solution(mesh):
    batch_axes = ("rep", "data")
    in_specs = (
        P(batch_axes, "model", None),
        P(batch_axes),
        P(None, "data"),
        P(None, "data", "model"),
        P(None, "data", None),
        P(None, "model", "data"),
    )
    return jax.shard_map(local_step, mesh=mesh, in_specs=in_specs, out_specs=P(batch_axes, "model", None), check_vma=False)
```

time: 2000 us -> 277 us (0.14); the launches traced: 1970 us -> 277 us
  waiting for transfers between devices: 924 us -> 0 us
  loops' own time: 339 us -> 0 us
  matrix products: 311 us -> 0 us
  local copies, waits for them, and re-layouts: 293 us -> 2.86 us
  Pallas kernels: 0 us -> 274 us
  other arithmetic: 80.4 us -> 0 us
    reduce_scatter x2 -> x0, waiting for transfers between devices: 738 us -> none  [local_step(): z_sum = lax.psum_scatter(z_part, 'model', scatter_dimension=1, tiled=True)]
    another operation x2 -> x0, loops' own time: 339 us -> none  [attend(): return lax.map(one_block, jnp.arange(n_blocks))]
    dot_general x264 -> x0, matrix products: 311 us -> none  [the longest x128 136 us: one_block(): jnp.einsum('cirl,cle->crie', attn_probs, values, preferred_element_type=j...]
    pallas_call x0 -> x1, Pallas kernels: none -> 274 us  [local_step(): pl.pallas_call(kernel, out_shape=jax.ShapeDtypeStruct(x.shape, x.dtype),...]
    all_gather x6 -> x0, waiting for transfers between devices: 185 us -> none  [the longest x2 166 us: local_step(): h_full = lax.all_gather(normed, 'model', axis=1, tiled=True)]
    dynamic_slice x256 -> x0, local copies, waits for them, and re-layouts: 176 us -> none  [the longest x128 101 us: one_block(): q_blk = lax.dynamic_index_in_dim(q_blocks, blk_idx, axis=1, keepdims=False)]
    dynamic_update_slice x128 -> x0, local copies, waits for them, and re-layouts: 78 us -> none  [attend(): return lax.map(one_block, jnp.arange(n_blocks))]
    sub x128 -> x0, other arithmetic: 41.7 us -> none  [one_block(): attn_probs = jax.nn.softmax(scores, axis=-1).astype(jnp.bfloat16)]
  transfers between devices with their start and end apart: 8 -> 0, of which waited for: 6 -> 0; matrix products, arithmetic and copies ran while one was open for 31% -> 0% of each run, Pallas kernels for 0% -> 0%
where the time goes in v1:
time: 277 us
  Pallas kernels  274 us (99%)
  local copies, waits for them, and re-layouts  2.86 us (1%)
    pallas_call x1, Pallas kernels, local_step(): pl.pallas_call(kernel, out_shape=jax.ShapeDtypeStruct(x.shape, x.dtype),...  274 us

profile of v1, /device:TPU:0, one launch (start us, length us, event | category | flops | bytes accessed | tf_op | source)
XLA Modules:
  0.0 276.7 jit_solution(5796609515870736633)
XLA Ops:
  0.0 1.3 copy.7.len_ref
  1.3 273.8 %layers.1 = bf16[2,32,1024]{2,1,0:T(8,128)(2,1)} custom-call(bf16[2,32,1024]{2,1,0:T(8,128)(2,1)} %x_ref.1, s32[2,1]{1,0:T(2,128)} %copy.7.len_ref, bf16[2,512]{1,0:T(2,128)(2,1)} %gamma_ref.1, bf16[2,512,2304]{2,1,0:T(8,128)(2,1)} %w_in_ref.1, bf16[2,512,256]{2,1,0:T(8,128)(2,1)} %w_kv_ref.1, bf16[2,1280,512]{2,1,0:T(8,128)(2,1)} %w_out_ref.1), custom_call_target="tpu_custom_call" | custom-call | tf_op jit(solution)/shard_map/layers/pallas_call | solution.py:418
  275.1 1.6 copy.9

commit v2 on v0

v2 whole, which is shorter than its diff:
```python
import functools

import jax
import jax.numpy as jnp
from jax import lax
from jax.experimental import pallas as pl
from jax.experimental.pallas import tpu as pltpu
from jax.sharding import PartitionSpec as P

EPSILON = 1e-6
MESH = pl.DeviceIdType.MESH
F32 = jnp.float32
BF16 = jnp.bfloat16

SIDE = 4
ROWS = 32
HALF = 16
D_MODEL = 1024
HEAD = 128
ATTN = 256
FF = 1024
TILE = SIDE * SIDE * HALF
N_TILES = SIDE
STRIDE = (16, 4, 1)
WIDTHS = (384, 384, 256)
AG_ORDER = ((2, 1, 0), (1, 0, 2), (0, 2, 1))
RS_ORDER = tuple(tuple(reversed(order)) for order in AG_ORDER)
NEG = -1e30
SEGMENT = 16
N_SEGMENTS = 4
LEAD, TRAIL = 10, 11
AG_STAGES = ((0, (0, 1, 2)), (1, (0, 1, 2)), (2, (0, 1)), (2, (3, 4)))
RS_STAGES = ((0, (3, 4)), (0, (0, 1)), (1, (0, 1, 2)), (2, (0, 1, 2)))
N_STAGES = 4


RS_AT = (0, 5, 11, 16, 20)
AG_AT = (-20, -17, -12, -6, 0)


def columns(half, part):
    order = [(i + half) % 3 for i in range(3)]
    lo = sum(WIDTHS[order[i]] for i in range(part))
    return lo, WIDTHS[order[part]]


def step_table():
    table = {}
    for half in range(2):
        for stage, at in enumerate(RS_AT):
            at += 24 + 8 * half
            table.setdefault(at % 32, []).append(("rs", half, stage, at // 32))
    for half in range(2):
        for stage, at in enumerate(AG_AT):
            at += 8 * half
            table.setdefault(at % 32, []).append(("ag", half, stage, at // 32))
    return table


def kernel(
    x_ref, len_ref, row_ref, column_ref, gamma_ref, w_in_ref, w_kv_ref, w_out_ref, y_ref,
    win, wkv, wout, gfull, hbuf, zbuf, xcur,
    ra, rb0, rb1, rb2,
    k_t, v_ext, q_ext, s_buf, p_buf, mixed,
    ag_send, ag_recv, rs_send, rs_recv, w_local, w_send, w_recv, g_local, g_send, g_recv,
):
    m = lax.axis_index("model")
    core = lax.axis_index("data")
    other = 1 - core
    pos = (lax.div(m, 16), lax.rem(lax.div(m, 4), 4), lax.rem(m, 4))
    rb = (rb0, rb1, rb2)

    def shift(axis, delta):
        return lax.rem(pos[axis] + delta + SIDE, SIDE)

    def neighbour(axis, delta):
        return {"model": m + (shift(axis, delta) - pos[axis]) * STRIDE[axis]}

    barrier = pltpu.get_barrier_semaphore()
    for axis in range(3):
        for delta in (1, -1, 2):
            pl.semaphore_signal(barrier, inc=1, device_id=neighbour(axis, delta), device_id_type=MESH)
    pl.semaphore_signal(barrier, inc=1, device_id={"data": other}, device_id_type=MESH)
    pl.semaphore_wait(barrier, 10)

    pairs = ((w_in_ref, win), (w_kv_ref, wkv), (w_out_ref, wout))

    def weight_local(layer, i):
        src, dst = pairs[i]
        return pltpu.make_async_copy(src.at[layer], dst.at[layer, core], w_local.at[layer, i])

    def weight_send(layer, i):
        src, dst = pairs[i]
        return pltpu.make_async_remote_copy(
            src_ref=src.at[layer], dst_ref=dst.at[layer, core], send_sem=w_send.at[layer, i],
            recv_sem=w_recv.at[layer, i], device_id={"data": other}, device_id_type=MESH)

    def weight_arrival(layer, i):
        src, dst = pairs[i]
        return pltpu.make_async_remote_copy(
            src_ref=src.at[layer], dst_ref=dst.at[layer, other], send_sem=w_send.at[layer, i],
            recv_sem=w_recv.at[layer, i], device_id={"data": other}, device_id_type=MESH)

    def weights_start(layer):
        for i in range(3):
            weight_send(layer, i).start()
            weight_local(layer, i).start()

    def weights_wait(layer):
        for i in range(3):
            weight_local(layer, i).wait()
            weight_send(layer, i).wait_send()
            weight_arrival(layer, i).wait_recv()

    gain_local = pltpu.make_async_copy(gamma_ref, gfull.at[core], g_local)
    gain_send = pltpu.make_async_remote_copy(
        src_ref=gamma_ref, dst_ref=gfull.at[core], send_sem=g_send, recv_sem=g_recv,
        device_id={"data": other}, device_id_type=MESH)
    gain_arrival = pltpu.make_async_remote_copy(
        src_ref=gamma_ref, dst_ref=gfull.at[other], send_sem=g_send, recv_sem=g_recv,
        device_id={"data": other}, device_id_type=MESH)
    gain_send.start()
    gain_local.start()
    weights_start(0)

    def split(where, lo, width, free, piece):
        where = list(where)
        if piece is not None:
            where[free[0]] = pl.ds(2 * piece, 2)
        return where, lo, width

    def h_block(b, half, part, phase, index, piece):
        order = AG_ORDER[part]
        where = [slice(None)] * 3
        for axis in order[phase + 1:]:
            where[axis] = pos[axis]
        where[order[phase]] = index
        where, lo, width = split(where, *columns(half, part), sorted(order[:phase]), piece)
        return hbuf.at[(b, half, *where, slice(None), pl.ds(lo, width))]

    def ag_copy(b, half, part, phase, slot, index, piece, delta):
        block = h_block(b, half, part, phase, index, piece)
        return pltpu.make_async_remote_copy(
            src_ref=block, dst_ref=block, send_sem=ag_send.at[2 * b + half, part, phase, slot],
            recv_sem=ag_recv.at[2 * b + half, part, phase, slot],
            device_id=neighbour(AG_ORDER[part][phase], delta), device_id_type=MESH)

    def ag_sent(b, half, part, phase, slot):
        axis = AG_ORDER[part][phase]
        index, piece, delta = ((pos[axis], None, 1), (pos[axis], None, -1), (pos[axis], None, 2),
                               (shift(axis, -1), 0, 1), (shift(axis, 1), 1, -1))[slot]
        return ag_copy(b, half, part, phase, slot, index, piece, delta)

    def ag_arrival(b, half, part, phase, slot):
        axis = AG_ORDER[part][phase]
        index, piece, delta = ((shift(axis, -1), None, 1), (shift(axis, 1), None, -1), (shift(axis, 2), None, 2),
                               (shift(axis, 2), 0, 1), (shift(axis, 2), 1, -1))[slot]
        return ag_copy(b, half, part, phase, slot, index, piece, delta)

    def ag_step(b, half, stage):
        for part in range(3):
            if stage:
                before, slots = AG_STAGES[stage - 1]
                for slot in slots:
                    ag_arrival(b, half, part, before, slot).wait_recv()
            if stage < N_STAGES:
                phase, slots = AG_STAGES[stage]
                for slot in slots:
                    ag_sent(b, half, part, phase, slot).start()
        if stage == N_STAGES:
            for part in range(3):
                for phase, slots in AG_STAGES:
                    for slot in slots:
                        ag_sent(b, half, part, phase, slot).wait_send()

    def z_where(part, phase, index):
        order = RS_ORDER[part]
        where = [slice(None)] * 3
        for axis in order[:phase]:
            where[axis] = pos[axis]
        where[order[phase]] = index
        return where, sorted(order[phase + 1:])

    def z_block(b, half, part, phase, index, piece):
        where, free = z_where(part, phase, index)
        where, lo, width = split(where, *columns(half, part), free, piece)
        return zbuf.at[(b, half, *where, slice(None), pl.ds(lo, width))]

    def rs_copy(b, half, part, phase, slot):
        axis = RS_ORDER[part][phase]
        piece = slot - 3 if slot >= 3 else None
        where, lo, width = split([slice(None)] * (2 - phase), *columns(half, part), list(range(2 - phase)), piece)
        cells = (*where, slice(None), pl.ds(lo, width))
        if slot >= 3:
            index, delta = shift(axis, 2), (-1, 1)[piece]
            dst = ra.at[(2 * b + half, *cells)]
        else:
            delta = (1, -1, 2)[slot]
            index = shift(axis, delta)
            dst = rb[phase].at[(2 * b + half, slot, *cells)]
        return pltpu.make_async_remote_copy(
            src_ref=z_block(b, half, part, phase, index, piece), dst_ref=dst,
            send_sem=rs_send.at[2 * b + half, part, phase, slot], recv_sem=rs_recv.at[2 * b + half, part, phase, slot],
            device_id=neighbour(axis, delta), device_id_type=MESH)

    def add_into(b, half, part, phase, index, piece, slots):
        where, free = z_where(part, phase, index)
        where, lo, width = split(where, *columns(half, part), free, piece)
        lead = [slice(None)] * len(free)
        if piece is not None:
            lead[0] = where[free[0]]
        target = (b, half, *where, slice(None), pl.ds(lo, width))
        cells = (*lead, slice(None), pl.ds(lo, width))
        total = zbuf[target].astype(F32)
        if piece is not None:
            total = total + ra[(2 * b + half, *cells)].astype(F32)
        for slot in slots:
            total = total + rb[phase][(2 * b + half, slot, *cells)].astype(F32)
        zbuf[target] = total.astype(BF16)

    def rs_step(b, half, stage):
        for part in range(3):
            if stage:
                before, slots = RS_STAGES[stage - 1]
                axis = RS_ORDER[part][before]
                for slot in slots:
                    rs_copy(b, half, part, before, slot).wait_recv()
                if stage == 1:
                    add_into(b, half, part, before, shift(axis, -1), 0, ())
                    add_into(b, half, part, before, shift(axis, 1), 1, ())
                else:
                    add_into(b, half, part, before, pos[axis], None, slots)
            if stage < N_STAGES:
                phase, slots = RS_STAGES[stage]
                for slot in slots:
                    rs_copy(b, half, part, phase, slot).start()
        if stage == N_STAGES:
            for part in range(3):
                for phase, slots in RS_STAGES:
                    for slot in slots:
                        rs_copy(b, half, part, phase, slot).wait_send()

    def norm(b, half, layer):
        x = xcur[b, half].astype(F32)
        gain = jnp.concatenate([gfull[0, layer:layer + 1, :], gfull[1, layer:layer + 1, :]], axis=1).astype(F32)
        inv = lax.rsqrt(jnp.mean(x * x, axis=-1, keepdims=True) + EPSILON)
        hbuf[b, half, pos[0], pos[1], pos[2]] = (x * inv * gain).astype(BF16)

    def residual(b, half):
        z = zbuf[b, half, pos[0], pos[1], pos[2]].astype(F32)
        xcur[b, half] = (xcur[b, half].astype(F32) + z).astype(BF16)

    for half in range(2):
        xcur[:, half] = x_ref[:, half * HALF:(half + 1) * HALF, :]
    gain_local.wait()
    gain_send.wait_send()
    gain_arrival.wait_recv()
    rows_i = lax.broadcasted_iota(jnp.int32, (HEAD, TILE), 0)
    q_ext[:, HEAD:] = jnp.where(lax.broadcasted_iota(jnp.int32, (2 * TILE, HEAD), 1) == 0, 1.0, 0.0).astype(BF16)
    v_ext[:, :, :, HEAD:] = jnp.ones((N_TILES, 2, TILE, HEAD), BF16)

    table = step_table()

    def run(kind, half, stage, seg):
        b = lax.rem(seg, 2)
        if kind == "rs":
            rs_step(b, half, stage)
            if stage == N_STAGES:
                residual(b, half)
        else:
            if stage == 0:
                @pl.when(seg < 2)
                def _():
                    norm(b, half, 0)

                @pl.when(seg >= 2)
                def _():
                    norm(b, half, 1)

            ag_step(b, half, stage)

    def tick(unit, point, lo=0, hi=SEGMENT):
        if not any(phase % 2 == point and lo <= phase // 2 < hi for phase in table):
            return
        place = lax.rem(unit, SEGMENT)
        if hi - lo == 1:
            for kind, half, stage, late in table[2 * lo + point]:
                seg = lax.div(unit, SEGMENT) - 2 - late

                @pl.when(jnp.logical_and(seg >= 0, seg < N_SEGMENTS))
                def _():
                    run(kind, half, stage, seg)
            return
        mid = (lo + hi) // 2

        @pl.when(place < mid)
        def _():
            tick(unit, point, lo, mid)

        @pl.when(place >= mid)
        def _():
            tick(unit, point, mid, hi)

    scale = float(HEAD ** -0.5 * 1.4426950408889634)

    def scores(head, t, half):
        rows = pl.ds(head * TILE, TILE)
        q = q_ext[rows, :]
        q_pos = column_ref[...] + half * HALF
        top = None
        for j in range(t + 1):
            for part in range(2):
                s = jnp.dot(q, k_t[j, part], preferred_element_type=F32)
                if j == t:
                    s = jnp.where(row_ref[...] + part * HALF <= q_pos, s, NEG)
                s_buf[rows, (2 * j + part) * TILE:(2 * j + part + 1) * TILE] = s
                high = jnp.maximum(s[:, :HEAD], s[:, HEAD:])
                top = high if top is None else jnp.maximum(top, high)
        return jnp.max(top, axis=-1, keepdims=True)

    def weigh(head, t, half, top):
        rows = pl.ds(head * TILE, TILE)
        n = 2 * (t + 1)
        for k in range(n):
            cells = (rows, pl.ds(k * TILE, TILE))
            p_buf[cells] = jnp.exp2((s_buf[cells] - top) * scale).astype(BF16)
        out = jnp.dot(
            p_buf[rows, :n * TILE], v_ext[:t + 1].reshape(n * TILE, 2 * HEAD), preferred_element_type=F32)
        mixed[half, t, :, head * HEAD:(head + 1) * HEAD] = (out[:, :HEAD] / out[:, HEAD:]).astype(BF16)

    def attend(t, half):
        tops = [scores(head, t, half) for head in range(2)]
        for head in range(2):
            weigh(head, t, half, tops[head])

    first = 2 * SEGMENT

    @pl.loop(first - LEAD, first + N_SEGMENTS * SEGMENT + TRAIL)
    def _(unit):
        seg = lax.div(unit, SEGMENT) - 2
        layer, b = lax.div(seg, 2), lax.rem(seg, 2)
        half, t = lax.rem(lax.div(unit, 4), 2), lax.rem(unit, 4)
        busy = jnp.logical_and(unit >= first, unit < first + N_SEGMENTS * SEGMENT)
        project = jnp.logical_and(busy, lax.rem(unit, SEGMENT) < 8)
        attention = jnp.logical_and(busy, lax.rem(unit, SEGMENT) >= 8)
        tick(unit, 0)

        @pl.when(unit == first)
        def _():
            weights_wait(0)
            weights_start(1)

        @pl.when(unit == first + 2 * SEGMENT)
        def _():
            weights_wait(1)

        def mlp(i):
            h = hbuf[b, half, t].reshape(TILE, D_MODEL)
            lo = ATTN + i * 512
            g = jnp.dot(h, win[layer, :, :, lo:lo + 512].reshape(D_MODEL, 512), preferred_element_type=F32)
            u = jnp.dot(h, win[layer, :, :, lo + FF:lo + FF + 512].reshape(D_MODEL, 512), preferred_element_type=F32)
            g = g.astype(BF16).astype(F32)
            u = u.astype(BF16).astype(F32)
            mixed[half, t, :, lo:lo + 512] = (jax.nn.silu(g) * u).astype(BF16)

        @pl.when(project)
        def _():
            h = hbuf[b, half, t].reshape(TILE, D_MODEL)
            kv = jnp.dot(h, wkv[layer].reshape(D_MODEL, 2 * HEAD), preferred_element_type=F32).astype(BF16)
            k_t[t, half, :HEAD, :] = kv[:, :HEAD].T
            key_pos = t * (2 * TILE) + half * HALF + row_ref[...]
            hidden = jnp.logical_and(rows_i == 0, key_pos >= len_ref[pl.ds(b, 1), :])
            k_t[t, half, HEAD:, :] = jnp.where(hidden, NEG, 0.0).astype(BF16)
            v_ext[t, half, :, :HEAD] = kv[:, HEAD:]
            mlp(0)

        @pl.when(attention)
        def _():
            h = hbuf[b, half, t].reshape(TILE, D_MODEL)
            q = jnp.dot(h, win[layer, :, :, :ATTN].reshape(D_MODEL, ATTN), preferred_element_type=F32).astype(BF16)
            q_ext[:TILE, :HEAD] = q[:, :HEAD]
            q_ext[TILE:, :HEAD] = q[:, HEAD:]
            for plane in range(N_TILES):
                @pl.when(t == plane)
                def _(plane=plane):
                    attend(plane, half)

        tick(unit, 1)

        @pl.when(project)
        def _():
            mlp(1)

        @pl.when(attention)
        def _():
            for side in range(2):
                z = jnp.dot(mixed[half, t], wout[layer, side], preferred_element_type=F32).astype(BF16)
                zbuf[b, half, t, :, :, :, side * 512:(side + 1) * 512] = z.reshape(SIDE, SIDE, HALF, 512)

    for half in range(2):
        y_ref[:, half * HALF:(half + 1) * HALF, :] = xcur[:, half]


def local_step(x, lengths, gamma, w_in, w_kv, w_out):
    vmem = pl.BlockSpec(memory_space=pltpu.VMEM)
    hbm = pl.BlockSpec(memory_space=pl.ANY)
    dma = pltpu.SemaphoreType.DMA
    box = (SIDE, SIDE)
    scratch = [
        pltpu.VMEM((2, 2, 512, 2304), BF16),
        pltpu.VMEM((2, 2, 512, 256), BF16),
        pltpu.VMEM((2, 2, 1280, 512), BF16),
        pltpu.VMEM((2, 2, 512), BF16),
        pltpu.VMEM((2, 2, SIDE, *box, HALF, D_MODEL), BF16),
        pltpu.VMEM((2, 2, SIDE, *box, HALF, D_MODEL), BF16),
        pltpu.VMEM((2, 2, HALF, D_MODEL), BF16),
        pltpu.VMEM((4, *box, HALF, D_MODEL), BF16),
        pltpu.VMEM((4, 2, *box, HALF, D_MODEL), BF16),
        pltpu.VMEM((4, 3, SIDE, HALF, D_MODEL), BF16),
        pltpu.VMEM((4, 3, HALF, D_MODEL), BF16),
        pltpu.VMEM((N_TILES, 2, 2 * HEAD, TILE), BF16),
        pltpu.VMEM((N_TILES, 2, TILE, 2 * HEAD), BF16),
        pltpu.VMEM((2 * TILE, 2 * HEAD), BF16),
        pltpu.VMEM((2 * TILE, 2 * N_TILES * TILE), F32),
        pltpu.VMEM((2 * TILE, 2 * N_TILES * TILE), BF16),
        pltpu.VMEM((2, N_TILES, TILE, ATTN + FF), BF16),
        dma((4, 3, 3, 5)), dma((4, 3, 3, 5)), dma((4, 3, 3, 5)), dma((4, 3, 3, 5)),
        dma((2, 3)), dma((2, 3)), dma((2, 3)), dma, dma, dma,
    ]
    place = jnp.asarray([i + HALF * (i // HALF) for i in range(TILE)], jnp.int32)
    return pl.pallas_call(
        kernel,
        out_shape=jax.ShapeDtypeStruct(x.shape, x.dtype),
        in_specs=[vmem] * 5 + [hbm] * 3,
        out_specs=vmem,
        scratch_shapes=scratch,
        compiler_params=pltpu.CompilerParams(
            collective_id=0, has_side_effects=True, vmem_limit_bytes=67_043_328),
        name="layers",
    )(x, lengths.reshape(2, 1), place[None], place[:, None], gamma, w_in, w_kv, w_out)


def solution(mesh):
    batch_axes = ("rep", "data")
    in_specs = (
        P(batch_axes, "model", None),
        P(batch_axes),
        P(None, "data"),
        P(None, "data", "model"),
        P(None, "data", None),
        P(None, "model", "data"),
    )
    return jax.shard_map(local_step, mesh=mesh, in_specs=in_specs, out_specs=P(batch_axes, "model", None), check_vma=False)
```

time: 2000 us -> 223 us (0.11); the launches traced: 1970 us -> 222 us
  waiting for transfers between devices: 924 us -> 0 us
  loops' own time: 339 us -> 0 us
  matrix products: 311 us -> 0 us
  local copies, waits for them, and re-layouts: 293 us -> 2.86 us
  Pallas kernels: 0 us -> 220 us
  other arithmetic: 80.4 us -> 0 us
    reduce_scatter x2 -> x0, waiting for transfers between devices: 738 us -> none  [local_step(): z_sum = lax.psum_scatter(z_part, 'model', scatter_dimension=1, tiled=True)]
    another operation x2 -> x0, loops' own time: 339 us -> none  [attend(): return lax.map(one_block, jnp.arange(n_blocks))]
    dot_general x264 -> x0, matrix products: 311 us -> none  [the longest x128 136 us: one_block(): jnp.einsum('cirl,cle->crie', attn_probs, values, preferred_element_type=j...]
    pallas_call x0 -> x1, Pallas kernels: none -> 220 us  [local_step(): pl.pallas_call(kernel, out_shape=jax.ShapeDtypeStruct(x.shape, x.dtype),...]
    all_gather x6 -> x0, waiting for transfers between devices: 185 us -> none  [the longest x2 166 us: local_step(): h_full = lax.all_gather(normed, 'model', axis=1, tiled=True)]
    dynamic_slice x256 -> x0, local copies, waits for them, and re-layouts: 176 us -> none  [the longest x128 101 us: one_block(): q_blk = lax.dynamic_index_in_dim(q_blocks, blk_idx, axis=1, keepdims=False)]
    dynamic_update_slice x128 -> x0, local copies, waits for them, and re-layouts: 78 us -> none  [attend(): return lax.map(one_block, jnp.arange(n_blocks))]
    sub x128 -> x0, other arithmetic: 41.7 us -> none  [one_block(): attn_probs = jax.nn.softmax(scores, axis=-1).astype(jnp.bfloat16)]
  transfers between devices with their start and end apart: 8 -> 0, of which waited for: 6 -> 0; matrix products, arithmetic and copies ran while one was open for 31% -> 0% of each run, Pallas kernels for 0% -> 0%
where the time goes in v2:
time: 223 us; the launch traced here: 222 us
  Pallas kernels  220 us (99%)
  local copies, waits for them, and re-layouts  2.86 us (1%)
    pallas_call x1, Pallas kernels, local_step(): pl.pallas_call(kernel, out_shape=jax.ShapeDtypeStruct(x.shape, x.dtype),...  220 us

profile of v2, /device:TPU:0, one launch (start us, length us, event | category | flops | bytes accessed | tf_op | source)
XLA Modules:
  0.0 222.5 jit_solution(18076501732543656678)
XLA Ops:
  0.0 1.3 copy.8.len_ref
  1.3 219.6 %layers.1 = bf16[2,32,1024]{2,1,0:T(8,128)(2,1)} custom-call(bf16[2,32,1024]{2,1,0:T(8,128)(2,1)} %x_ref.1, s32[2,1]{1,0:T(2,128)} %copy.8.len_ref, s32[1,256]{1,0:T(1,128)} %constant.4.row_ref, s32[256,1]{1,0:T(8,128)} %constant.5.column_ref, bf16[2,512]{1,0:T(2,128)(2,1)} %gamma_ref.1, bf16[2,512,2304]{2,1,0:T(8,128)(2,1)} %w_in_ref.1, ...), custom_call_target="tpu_custom_call" | custom-call | tf_op jit(solution)/shard_map/layers/pallas_call | solution.py:431
  220.9 1.6 copy.10

commit v3 on v2

--- a/solution.py
+++ b/solution.py
@@ -22,26 +22,27 @@
 TILE = SIDE * SIDE * HALF
 N_TILES = SIDE
 STRIDE = (16, 4, 1)
-WIDTHS = (384, 384, 256)
 AG_ORDER = ((2, 1, 0), (1, 0, 2), (0, 2, 1))
 RS_ORDER = tuple(tuple(reversed(order)) for order in AG_ORDER)
 NEG = -1e30
 SEGMENT = 16
 N_SEGMENTS = 4
-LEAD, TRAIL = 10, 11
-AG_STAGES = ((0, (0, 1, 2)), (1, (0, 1, 2)), (2, (0, 1)), (2, (3, 4)))
-RS_STAGES = ((0, (3, 4)), (0, (0, 1)), (1, (0, 1, 2)), (2, (0, 1, 2)))
+LEAD, TRAIL = 12, 12
+AG_SENDS = ((0, (0, 1, 2)), (1, (0, 1, 2)), (2, (5, 7, 6, 8)), (2, (3, 4)))
+AG_WAITS = ((0, (0, 1, 2)), (1, (0, 1, 2)), (2, (5, 7)), (2, (6, 8, 3, 4)))
+RS_SENDS = ((0, (3, 4, 5, 6)), (0, (7, 8)), (1, (0, 1, 2)), (2, (0, 1, 2)))
+RS_WAITS = ((0, (3, 4)), (0, (5, 6, 7, 8)), (1, (0, 1, 2)), (2, (0, 1, 2)))
 N_STAGES = 4
 
 
-RS_AT = (0, 5, 11, 16, 20)
-AG_AT = (-20, -17, -12, -6, 0)
-
-
-def columns(half, part):
-    order = [(i + half) % 3 for i in range(3)]
-    lo = sum(WIDTHS[order[i]] for i in range(part))
-    return lo, WIDTHS[order[part]]
+RS_AT = (0, 5, 10, 15, 20)
+AG_AT = (-20, -16, -11, -6, 0)
+
+
+def columns(kind, half, part):
+    widths = [384] * 3
+    widths[{"ag": (2, 1), "rs": (0, 2)}[kind][half]] = 256
+    return sum(widths[:part]), widths[part]
 
 
 def step_table():
@@ -135,7 +136,7 @@
         for axis in order[phase + 1:]:
             where[axis] = pos[axis]
         where[order[phase]] = index
-        where, lo, width = split(where, *columns(half, part), sorted(order[:phase]), piece)
+        where, lo, width = split(where, *columns("ag", half, part), sorted(order[:phase]), piece)
         return hbuf.at[(b, half, *where, slice(None), pl.ds(lo, width))]
 
     def ag_copy(b, half, part, phase, slot, index, piece, delta):
@@ -148,28 +149,31 @@
     def ag_sent(b, half, part, phase, slot):
         axis = AG_ORDER[part][phase]
         index, piece, delta = ((pos[axis], None, 1), (pos[axis], None, -1), (pos[axis], None, 2),
-                               (shift(axis, -1), 0, 1), (shift(axis, 1), 1, -1))[slot]
+                               (shift(axis, -1), 0, 1), (shift(axis, 1), 1, -1),
+                               (pos[axis], 0, 1), (pos[axis], 1, 1), (pos[axis], 1, -1), (pos[axis], 0, -1))[slot]
         return ag_copy(b, half, part, phase, slot, index, piece, delta)
 
     def ag_arrival(b, half, part, phase, slot):
         axis = AG_ORDER[part][phase]
         index, piece, delta = ((shift(axis, -1), None, 1), (shift(axis, 1), None, -1), (shift(axis, 2), None, 2),
-                               (shift(axis, 2), 0, 1), (shift(axis, 2), 1, -1))[slot]
+                               (shift(axis, 2), 0, 1), (shift(axis, 2), 1, -1),
+                               (shift(axis, -1), 0, 1), (shift(axis, -1), 1, 1),
+                               (shift(axis, 1), 1, -1), (shift(axis, 1), 0, -1))[slot]
         return ag_copy(b, half, part, phase, slot, index, piece, delta)
 
     def ag_step(b, half, stage):
         for part in range(3):
             if stage:
-                before, slots = AG_STAGES[stage - 1]
+                before, slots = AG_WAITS[stage - 1]
                 for slot in slots:
                     ag_arrival(b, half, part, before, slot).wait_recv()
             if stage < N_STAGES:
-                phase, slots = AG_STAGES[stage]
+                phase, slots = AG_SENDS[stage]
                 for slot in slots:
                     ag_sent(b, half, part, phase, slot).start()
         if stage == N_STAGES:
             for part in range(3):
-                for phase, slots in AG_STAGES:
+                for phase, slots in AG_SENDS:
                     for slot in slots:
                         ag_sent(b, half, part, phase, slot).wait_send()
 
@@ -183,21 +187,20 @@
 
     def z_block(b, half, part, phase, index, piece):
         where, free = z_where(part, phase, index)
-        where, lo, width = split(where, *columns(half, part), free, piece)
+        where, lo, width = split(where, *columns("rs", half, part), free, piece)
         return zbuf.at[(b, half, *where, slice(None), pl.ds(lo, width))]
 
     def rs_copy(b, half, part, phase, slot):
         axis = RS_ORDER[part][phase]
-        piece = slot - 3 if slot >= 3 else None
-        where, lo, width = split([slice(None)] * (2 - phase), *columns(half, part), list(range(2 - phase)), piece)
+        ahead, piece, delta = ((1, None, 1), (-1, None, -1), (2, None, 2), (2, 0, -1), (2, 1, 1),
+                               (-1, 1, -1), (1, 0, 1), (-1, 0, -1), (1, 1, 1))[slot]
+        index = shift(axis, ahead)
+        where, lo, width = split([slice(None)] * (2 - phase), *columns("rs", half, part), list(range(2 - phase)), piece)
         cells = (*where, slice(None), pl.ds(lo, width))
-        if slot >= 3:
-            index, delta = shift(axis, 2), (-1, 1)[piece]
+        if ahead == 2 and delta != 2:
             dst = ra.at[(2 * b + half, *cells)]
         else:
-            delta = (1, -1, 2)[slot]
-            index = shift(axis, delta)
-            dst = rb[phase].at[(2 * b + half, slot, *cells)]
+            dst = rb[phase].at[(2 * b + half, {1: 0, -1: 1, 2: 2}[delta], *cells)]
         return pltpu.make_async_remote_copy(
             src_ref=z_block(b, half, part, phase, index, piece), dst_ref=dst,
             send_sem=rs_send.at[2 * b + half, part, phase, slot], recv_sem=rs_recv.at[2 * b + half, part, phase, slot],
@@ -205,7 +208,7 @@
 
     def add_into(b, half, part, phase, index, piece, slots):
         where, free = z_where(part, phase, index)
-        where, lo, width = split(where, *columns(half, part), free, piece)
+        where, lo, width = split(where, *columns("rs", half, part), free, piece)
         lead = [slice(None)] * len(free)
         if piece is not None:
             lead[0] = where[free[0]]
@@ -221,22 +224,22 @@
     def rs_step(b, half, stage):
         for part in range(3):
             if stage:
-                before, slots = RS_STAGES[stage - 1]
+                before, slots = RS_WAITS[stage - 1]
                 axis = RS_ORDER[part][before]
                 for slot in slots:
                     rs_copy(b, half, part, before, slot).wait_recv()
-                if stage == 1:
+                if slots == (3, 4):
                     add_into(b, half, part, before, shift(axis, -1), 0, ())
                     add_into(b, half, part, before, shift(axis, 1), 1, ())
                 else:
-                    add_into(b, half, part, before, pos[axis], None, slots)
+                    add_into(b, half, part, before, pos[axis], None, slots if before else (0, 1))
             if stage < N_STAGES:
-                phase, slots = RS_STAGES[stage]
+                phase, slots = RS_SENDS[stage]
                 for slot in slots:
                     rs_copy(b, half, part, phase, slot).start()
         if stage == N_STAGES:
             for part in range(3):
-                for phase, slots in RS_STAGES:
+                for phase, slots in RS_SENDS:
                     for slot in slots:
                         rs_copy(b, half, part, phase, slot).wait_send()
 
@@ -256,7 +259,10 @@
     gain_send.wait_send()
     gain_arrival.wait_recv()
     rows_i = lax.broadcasted_iota(jnp.int32, (HEAD, TILE), 0)
-    q_ext[:, HEAD:] = jnp.where(lax.broadcasted_iota(jnp.int32, (2 * TILE, HEAD), 1) == 0, 1.0, 0.0).astype(BF16)
+    ones = jnp.where(lax.broadcasted_iota(jnp.int32, (2 * TILE, HEAD), 1) == 0, 1.0, 0.0).astype(BF16)
+    for half in range(2):
+        for t in range(N_TILES):
+            q_ext[half, t, :, HEAD:] = ones
     v_ext[:, :, :, HEAD:] = jnp.ones((N_TILES, 2, TILE, HEAD), BF16)
 
     table = step_table()
@@ -305,7 +311,7 @@
 
     def scores(head, t, half):
         rows = pl.ds(head * TILE, TILE)
-        q = q_ext[rows, :]
+        q = q_ext[half, t, rows, :]
         q_pos = column_ref[...] + half * HALF
         top = None
         for j in range(t + 1):
@@ -354,32 +360,42 @@
         def _():
             weights_wait(1)
 
+        even = lax.rem(t, 2) == 0
+        pair = pl.ds(t - lax.rem(t, 2), 2)
+
+        def normed():
+            return hbuf[b, half, pair].reshape(2 * TILE, D_MODEL)
+
         def mlp(i):
-            h = hbuf[b, half, t].reshape(TILE, D_MODEL)
+            h = normed()
             lo = ATTN + i * 512
             g = jnp.dot(h, win[layer, :, :, lo:lo + 512].reshape(D_MODEL, 512), preferred_element_type=F32)
             u = jnp.dot(h, win[layer, :, :, lo + FF:lo + FF + 512].reshape(D_MODEL, 512), preferred_element_type=F32)
             g = g.astype(BF16).astype(F32)
             u = u.astype(BF16).astype(F32)
-            mixed[half, t, :, lo:lo + 512] = (jax.nn.silu(g) * u).astype(BF16)
-
-        @pl.when(project)
-        def _():
-            h = hbuf[b, half, t].reshape(TILE, D_MODEL)
-            kv = jnp.dot(h, wkv[layer].reshape(D_MODEL, 2 * HEAD), preferred_element_type=F32).astype(BF16)
-            k_t[t, half, :HEAD, :] = kv[:, :HEAD].T
-            key_pos = t * (2 * TILE) + half * HALF + row_ref[...]
-            hidden = jnp.logical_and(rows_i == 0, key_pos >= len_ref[pl.ds(b, 1), :])
-            k_t[t, half, HEAD:, :] = jnp.where(hidden, NEG, 0.0).astype(BF16)
-            v_ext[t, half, :, :HEAD] = kv[:, HEAD:]
-            mlp(0)
+            mixed[half, pair, :, lo:lo + 512] = (jax.nn.silu(g) * u).astype(BF16).reshape(2, TILE, 512)
+
+        @pl.when(jnp.logical_and(project, even))
+        def _():
+            kv = jnp.dot(normed(), wkv[layer].reshape(D_MODEL, 2 * HEAD), preferred_element_type=F32).astype(BF16)
+            q = jnp.dot(
+                normed(), win[layer, :, :, :ATTN].reshape(D_MODEL, ATTN), preferred_element_type=F32).astype(BF16)
+            for k in range(2):
+                rows = slice(k * TILE, (k + 1) * TILE)
+                k_t[t + k, half, :HEAD, :] = kv[rows, :HEAD].T
+                key_pos = (t + k) * (2 * TILE) + half * HALF + row_ref[...]
+                hidden = jnp.logical_and(rows_i == 0, key_pos >= len_ref[pl.ds(b, 1), :])
+                k_t[t + k, half, HEAD:, :] = jnp.where(hidden, NEG, 0.0).astype(BF16)
+                v_ext[t + k, half, :, :HEAD] = kv[rows, HEAD:]
+                q_ext[half, t + k, :TILE, :HEAD] = q[rows, :HEAD]
+                q_ext[half, t + k, TILE:, :HEAD] = q[rows, HEAD:]
+
+        @pl.when(jnp.logical_and(project, lax.rem(t, 2) == 1))
+        def _():
+            mlp(1)
 
         @pl.when(attention)
         def _():
-            h = hbuf[b, half, t].reshape(TILE, D_MODEL)
-            q = jnp.dot(h, win[layer, :, :, :ATTN].reshape(D_MODEL, ATTN), preferred_element_type=F32).astype(BF16)
-            q_ext[:TILE, :HEAD] = q[:, :HEAD]
-            q_ext[TILE:, :HEAD] = q[:, HEAD:]
             for plane in range(N_TILES):
                 @pl.when(t == plane)
                 def _(plane=plane):
@@ -387,15 +403,16 @@
 
         tick(unit, 1)
 
-        @pl.when(project)
-        def _():
-            mlp(1)
-
-        @pl.when(attention)
+        @pl.when(jnp.logical_and(project, even))
+        def _():
+            mlp(0)
+
+        @pl.when(jnp.logical_and(attention, lax.rem(t, 2) == 1))
         def _():
             for side in range(2):
-                z = jnp.dot(mixed[half, t], wout[layer, side], preferred_element_type=F32).astype(BF16)
-                zbuf[b, half, t, :, :, :, side * 512:(side + 1) * 512] = z.reshape(SIDE, SIDE, HALF, 512)
+                z = jnp.dot(
+                    mixed[half, pair].reshape(2 * TILE, ATTN + FF), wout[layer, side], preferred_element_type=F32)
+                zbuf[b, half, pair, :, :, :, side * 512:(side + 1) * 512] = z.astype(BF16).reshape(2, SIDE, SIDE, HALF, 512)
 
     for half in range(2):
         y_ref[:, half * HALF:(half + 1) * HALF, :] = xcur[:, half]
@@ -420,11 +437,11 @@
         pltpu.VMEM((4, 3, HALF, D_MODEL), BF16),
         pltpu.VMEM((N_TILES, 2, 2 * HEAD, TILE), BF16),
         pltpu.VMEM((N_TILES, 2, TILE, 2 * HEAD), BF16),
-        pltpu.VMEM((2 * TILE, 2 * HEAD), BF16),
+        pltpu.VMEM((2, N_TILES, 2 * TILE, 2 * HEAD), BF16),
         pltpu.VMEM((2 * TILE, 2 * N_TILES * TILE), F32),
         pltpu.VMEM((2 * TILE, 2 * N_TILES * TILE), BF16),
         pltpu.VMEM((2, N_TILES, TILE, ATTN + FF), BF16),
-        dma((4, 3, 3, 5)), dma((4, 3, 3, 5)), dma((4, 3, 3, 5)), dma((4, 3, 3, 5)),
+        dma((4, 3, 3, 9)), dma((4, 3, 3, 9)), dma((4, 3, 3, 9)), dma((4, 3, 3, 9)),
         dma((2, 3)), dma((2, 3)), dma((2, 3)), dma, dma, dma,
     ]
     place = jnp.asarray([i + HALF * (i // HALF) for i in range(TILE)], jnp.int32)

time: 223 us -> 215 us (0.964)
  Pallas kernels: 220 us -> 212 us
    pallas_call x1, Pallas kernels: 220 us -> 212 us  [local_step(): pl.pallas_call(kernel, out_shape=jax.ShapeDtypeStruct(x.shape, x.dtype),...]
where the time goes in v3:
time: 215 us
  Pallas kernels  212 us (99%)
  local copies, waits for them, and re-layouts  2.86 us (1%)
    pallas_call x1, Pallas kernels, local_step(): pl.pallas_call(kernel, out_shape=jax.ShapeDtypeStruct(x.shape, x.dtype),...  212 us

profile of v3, /device:TPU:0, one launch (start us, length us, event | category | flops | bytes accessed | tf_op | source)
XLA Modules:
  0.0 214.6 jit_solution(5435121085717769572)
XLA Ops:
  0.0 1.3 copy.8.len_ref
  1.3 211.7 %layers.1 = bf16[2,32,1024]{2,1,0:T(8,128)(2,1)} custom-call(bf16[2,32,1024]{2,1,0:T(8,128)(2,1)} %x_ref.1, s32[2,1]{1,0:T(2,128)} %copy.8.len_ref, s32[1,256]{1,0:T(1,128)} %constant.4.row_ref, s32[256,1]{1,0:T(8,128)} %constant.5.column_ref, bf16[2,512]{1,0:T(2,128)(2,1)} %gamma_ref.1, bf16[2,512,2304]{2,1,0:T(8,128)(2,1)} %w_in_ref.1, ...), custom_call_target="tpu_custom_call" | custom-call | tf_op jit(solution)/shard_map/layers/pallas_call | solution.py:448
  213.0 1.6 copy.10

commit v4 on v3

--- a/solution.py
+++ b/solution.py
@@ -27,7 +27,7 @@
 NEG = -1e30
 SEGMENT = 16
 N_SEGMENTS = 4
-LEAD, TRAIL = 12, 12
+LEAD, TRAIL = 10, 11
 AG_SENDS = ((0, (0, 1, 2)), (1, (0, 1, 2)), (2, (5, 7, 6, 8)), (2, (3, 4)))
 AG_WAITS = ((0, (0, 1, 2)), (1, (0, 1, 2)), (2, (5, 7)), (2, (6, 8, 3, 4)))
 RS_SENDS = ((0, (3, 4, 5, 6)), (0, (7, 8)), (1, (0, 1, 2)), (2, (0, 1, 2)))
@@ -55,6 +55,9 @@
         for stage, at in enumerate(AG_AT):
             at += 8 * half
             table.setdefault(at % 32, []).append(("ag", half, stage, at // 32))
+    for steps in table.values():
+        if steps[0][0] == "rs" and steps[0][2] == 0 and steps[-1][0] == "ag" and steps[-1][2] < N_STAGES:
+            steps.reverse()
     return table
 
 
@@ -122,7 +125,6 @@
         device_id={"data": other}, device_id_type=MESH)
     gain_send.start()
     gain_local.start()
-    weights_start(0)
 
     def split(where, lo, width, free, piece):
         where = list(where)
@@ -350,6 +352,10 @@
         project = jnp.logical_and(busy, lax.rem(unit, SEGMENT) < 8)
         attention = jnp.logical_and(busy, lax.rem(unit, SEGMENT) >= 8)
         tick(unit, 0)
+
+        @pl.when(unit == first - LEAD)
+        def _():
+            weights_start(0)
 
         @pl.when(unit == first)
         def _():

time: 215 us -> 216 us (level)
  no operation moved by 1% of the time
where the time goes in v4:
time: 216 us
  Pallas kernels  213 us (99%)
  local copies, waits for them, and re-layouts  2.86 us (1%)
    pallas_call x1, Pallas kernels, local_step(): pl.pallas_call(kernel, out_shape=jax.ShapeDtypeStruct(x.shape, x.dtype),...  213 us

profile of v4, /device:TPU:0, one launch (start us, length us, event | category | flops | bytes accessed | tf_op | source)
XLA Modules:
  0.0 215.7 jit_solution(3577328257167615642)
XLA Ops:
  0.0 1.3 copy.8.len_ref
  1.3 212.8 %layers.1 = bf16[2,32,1024]{2,1,0:T(8,128)(2,1)} custom-call(bf16[2,32,1024]{2,1,0:T(8,128)(2,1)} %x_ref.1, s32[2,1]{1,0:T(2,128)} %copy.8.len_ref, s32[1,256]{1,0:T(1,128)} %constant.4.row_ref, s32[256,1]{1,0:T(8,128)} %constant.5.column_ref, bf16[2,512]{1,0:T(2,128)(2,1)} %gamma_ref.1, bf16[2,512,2304]{2,1,0:T(8,128)(2,1)} %w_in_ref.1, ...), custom_call_target="tpu_custom_call" | custom-call | tf_op jit(solution)/shard_map/layers/pallas_call | solution.py:454
  214.1 1.6 copy.10
